TPU v7x, 32 devices: a whole 2x2x4 slice. The times are simulated.
32 devices in a mesh: seq: 16 (over z, y, core), grp: 2 (over x).
Axes of the slice: x: 2, y: 2, z: 4, core: 2. Of those that a mesh axis runs over, the one named last changes fastest.
Arguments:
- queries: bfloat16 [4096, 3584], P(('grp', 'seq')), parts along dimension 0, may hold values from -5 to 5
- keys: bfloat16 [4096, 512], P(('grp', 'seq')), parts along dimension 0, may hold values from -5 to 5
- values: bfloat16 [4096, 512], P(('grp', 'seq')), parts along dimension 0, may hold values from -6 to 6
- doc_lengths: int32 [16], P('grp'), parts along dimension 0, may hold values from 1 to 1280, 2048 in all
Outputs:
- attended: bfloat16 [4096, 3584], P(('grp', 'seq')), parts along dimension 0
There are 2 independent parts, one for each index of `grp`. A program takes and returns all parts, laid end to end along the dimension named above; each array names one. Nothing has to cross between parts.
Inputs may be any that keep to these rules, and one draw needn't show every extreme that they name: `doc_lengths`: the 8 documents lie one after another and their lengths sum to 2048; the longest has exactly 1280 tokens.
All inputs are finite; a program needn't handle non-finite values.
Results may differ from a plain program's by a relative error of at most 0.0085.
Values may be sent and summed in bfloat16 or wider, within the bound.
No kernel may reach another device: no remote copies, remote signals or barrier semaphores. Data moves between devices by JAX's collectives and lax.ppermute only.
A program may use at most 192 MiB of HBM per device.

v0:
```python
import jax
import jax.numpy as jnp
from jax import lax
from jax.sharding import PartitionSpec as P

HEADS = 28
KV_HEADS = 4
HEAD_DIM = 128
rope_base = 1000000.0
negative = -1e30


def doc_place(position, doc_lengths):
    doc_ends = jnp.cumsum(doc_lengths)
    beyond = position[:, None] >= doc_ends[None, :]
    doc_index = jnp.sum(beyond.astype(jnp.int32), axis=1)
    doc_start = jnp.sum(jnp.where(beyond, doc_lengths[None, :], 0), axis=1)
    return (doc_index, doc_start)


def rotate(values_in, within_doc, head_count):
    row_count = values_in.shape[0]
    half_dim = HEAD_DIM // 2
    inverse_freq = jnp.power(
        jnp.float32(rope_base), -2.0 * jnp.arange(half_dim, dtype=jnp.float32) / HEAD_DIM
    )
    angles = within_doc.astype(jnp.float32)[:, None] * inverse_freq[None, :]
    cosine = jnp.cos(angles)[:, None, :]
    sines = jnp.sin(angles)[:, None, :]
    fields = values_in.astype(jnp.float32).reshape(row_count, head_count, HEAD_DIM)
    lower_half = fields[..., :half_dim]
    upper_half = fields[..., half_dim:]
    rotated = jnp.concatenate(
        [lower_half * cosine - upper_half * sines, upper_half * cosine + lower_half * sines],
        axis=-1,
    )
    return rotated.reshape(row_count, head_count * HEAD_DIM).astype(jnp.bfloat16)


def per_device(queries, keys, values, doc_lengths):
    row_count = queries.shape[0]
    dev_index = lax.axis_index("seq")
    group_size = HEADS // KV_HEADS
    score_scale = HEAD_DIM ** (-0.5)
    local_rows = jnp.arange(row_count, dtype=jnp.int32)
    own_pos = dev_index * row_count + local_rows
    own_start = doc_place(own_pos, doc_lengths)[1]
    within_doc = own_pos - own_start
    q_rot = rotate(queries, within_doc, HEADS)
    k_rot = rotate(keys, within_doc, KV_HEADS)
    query_doc = doc_place(own_pos, doc_lengths)[0]
    q_heads = q_rot.reshape(row_count, KV_HEADS, group_size, HEAD_DIM)
    k_piece = lax.all_gather(k_rot, "seq", axis=0, tiled=True)
    v_piece = lax.all_gather(values, "seq", axis=0, tiled=True)
    length = k_piece.shape[0]
    key_pos = jnp.arange(length, dtype=jnp.int32)
    key_doc = doc_place(key_pos, doc_lengths)[0]
    allowed = (key_doc[None, :] == query_doc[:, None]) & (key_pos[None, :] <= own_pos[:, None])
    allowed_wide = allowed[:, None, None, :]
    running_max = jnp.full((row_count, KV_HEADS, group_size), negative, jnp.float32)
    k_heads = k_piece.reshape(length, KV_HEADS, HEAD_DIM)
    v_heads = v_piece.reshape(length, KV_HEADS, HEAD_DIM)
    scores = (
        jnp.einsum("qkgd,skd->qkgs", q_heads, k_heads, preferred_element_type=jnp.float32)
        * score_scale
    )
    scores = jnp.where(allowed_wide, scores, negative)
    new_max = jnp.maximum(running_max, jnp.max(scores, axis=-1))
    weight = jnp.where(allowed_wide, jnp.exp(scores - new_max[..., None]), 0.0)
    weight_sum = jnp.sum(weight, axis=-1)
    weighted = jnp.einsum(
        "qkgs,skd->qkgd", weight.astype(jnp.bfloat16), v_heads, preferred_element_type=jnp.float32
    )
    running_max, weight_sum, weighted = (new_max, weight_sum, weighted)
    attended = (
        (weighted / weight_sum[..., None]).reshape(row_count, HEADS * HEAD_DIM).astype(jnp.bfloat16)
    )
    return attended


def solution(mesh):
    return jax.shard_map(
        per_device,
        mesh=mesh,
        in_specs=(
            P(("grp", "seq"), None),
            P(("grp", "seq"), None),
            P(("grp", "seq"), None),
            P("grp"),
        ),
        out_specs=P(("grp", "seq"), None),
        check_vma=False,
    )
```

profile of v0, /device:TPU:0, one launch (start us, length us, event | category | flops | bytes accessed | tf_op | source)
XLA Modules:
  0.0 121.0 jit_solution(10799247144488770682)
XLA Ops:
  6.5 0.0 all-gather.3.cloned.1.call-start
  6.6 0.8 reduce-window.8
  7.4 0.7 fusion.10
  8.2 1.0 copy.31
  9.2 0.2 multiply_cosine_fusion
  9.4 0.7 pad_maximum_fusion.1
  10.1 0.0 all-gather.3.cloned.1.call-update
  10.1 0.0 all-gather.5.cloned.1.call-start
  10.1 0.7 all-gather.5.cloned.1.call-update
  10.9 0.1 convert_reduce_fusion
  10.9 1.6 %copy.20 = bf16[128,3584]{0,1:T(8,128)(2,1)S(1)} copy(bf16[128,3584]{1,0:T(8,128)(2,1)} %param.4) | data formatting | bytes 1835008 | tf_op args[0]
  12.5 0.2 convert.18
  12.7 0.3 fusion.9
  13.1 0.3 subtract_convert_fusion
  13.3 0.1 pad_maximum_fusion
  13.4 40.6 %all-gather.3.cloned.1.call-done = bf16[2048,512]{0,1:T(8,128)(2,1)} async-done(((bf16[128,512]{0,1:T(8,128)(2,1)}), bf16[2048,512]{0,1:T(8,128)(2,1)}) %all-gather.3.cloned.1.call-update) | async-done | bytes 2097168 | tf_op jit(solution)/shard_map/all_gather | solution.py:53
  54.0 13.3 %fusion = (f32[128,4,7]{0,2,1:T(8,128)S(1)}, f32[4,2048,128,7]{2,1,3,0:T(8,128)}) fusion(pred[128,2048]{0,1:T(8,128)(4,1)S(1)} %fusion.9, bf16[2048,4,128,1]{0,2,3,1:T(8,128)(2,1)} %bitcast.42, bf16[128,4,7,128]{0,3,2,1:T(8,128)(2,1)S(1)} %bitcast.40), kind=kOutput, calls=%fused_computation.2 | convolution fusion | flops 1901064704 | bytes 32651264 | tf_op jit(solution)/shard_map/qkgd,skd->qkgs/dot_general | solution.py:64
  67.4 13.2 %fusion.1 = f32[128,4,7]{0,2,1:T(8,128)S(1)} fusion(f32[4,2048,128,7]{2,1,3,0:T(8,128)} %get-tuple-element.14, f32[128,4,7]{0,2,1:T(8,128)S(1)} %broadcast_maximum_fusion, pred[128,2048]{0,1:T(8,128)(4,1)S(1)} %fusion.9), kind=kLoop, calls=%fused_computation.3 | loop fusion | flops 36696576 | bytes 29650944 | tf_op jit(solution)/shard_map/reduce_sum | solution.py:70
  80.6 16.2 %all-gather.5.cloned.1.call-done = bf16[2048,512]{1,0:T(8,128)(2,1)} async-done(((bf16[128,512]{1,0:T(8,128)(2,1)}), bf16[2048,512]{1,0:T(8,128)(2,1)}) %all-gather.5.cloned.1.call-update) | async-done | bytes 2097168 | tf_op jit(solution)/shard_map/all_gather | solution.py:54
  96.8 2.9 %copy.23 = bf16[2048,512]{0,1:T(8,128)(2,1)S(1)} copy(bf16[2048,512]{1,0:T(8,128)(2,1)} %all-gather.5.cloned.1.call-done) | data formatting | bytes 4194304 | tf_op jit(solution)/shard_map/all_gather | solution.py:54
  99.7 13.2 %fusion.6 = bf16[128,4,7,128]{0,3,2,1:T(8,128)(2,1)S(1)} fusion(bf16[2048,4,128,1]{0,2,3,1:T(8,128)(2,1)S(1)} %bitcast.41, f32[4,2048,128,7]{2,1,3,0:T(8,128)} %get-tuple-element.14, f32[128,4,7]{0,2,1:T(8,128)S(1)} %broadcast_maximum_fusion, pred[128,2048]{0,1:T(8,128)(4,1)S(1)} %fusion.9, f32[128,4,7]{0,2,1:T(8,128)S(1)} %fusion.1), kind=kOutput, calls=%fused_computation.8 | convolution fusion | flops 1916665856 | bytes 32665600 | tf_op jit(solution)/shard_map/qkgs,skd->qkgd/dot_general | solution.py:71
  112.9 1.3 %copy.25 = bf16[128,3584]{1,0:T(8,128)(2,1)} copy(bf16[128,3584]{0,1:T(8,128)(2,1)S(1)} %bitcast.44) | data formatting | bytes 1835008 | tf_op jit(solution)/shard_map/convert_element_type | solution.py:76
  (5 shorter events, 0.1 us)
Async XLA Ops:
  6.5 47.5 %all-gather.3.cloned.1.call-start = ((), (), s32[]{:S(2)}) async-start(), calls=%async_computation | async-start | bytes 2228224 | tf_op jit(solution)/shard_map/all_gather | solution.py:53
  10.1 86.7 %all-gather.5.cloned.1.call-start = ((), (), s32[]{:S(2)}) async-start(), calls=%async_computation.1 | async-start | bytes 2228224 | tf_op jit(solution)/shard_map/all_gather | solution.py:54
Sparse Core Ops, SparseCore 0:
  10.2 43.7 all-gather.2
  56.2 40.5 all-gather.4
where the time goes:
time: 121 us
  waiting for transfers between devices  57.5 us (48%)
  matrix products  26.5 us (22%)
  other arithmetic  16.7 us (14%)
  between operations  13.5 us (11%)
  local copies, waits for them, and re-layouts  6.76 us (6%)
    all_gather x1, waiting for transfers between devices, per_device(): k_piece = lax.all_gather(k_rot, 'seq', axis=0, tiled=True)  40.6 us
    all_gather x1, waiting for transfers between devices, per_device(): v_piece = lax.all_gather(values, 'seq', axis=0, tiled=True)  16.2 us
    dot_general x1, matrix products, per_device(): jnp.einsum('qkgd,skd->qkgs', q_heads, k_heads, preferred_element_type=jnp...  13.3 us
    reduce_sum x1, other arithmetic, per_device(): weight_sum = jnp.sum(weight, axis=-1)  13.2 us
    dot_general x1, matrix products, per_device(): jnp.einsum('qkgs,skd->qkgd', weight.astype(jnp.bfloat16), v_heads, prefer...  13.2 us
    all_gather x1, local copies, waits for them, and re-layouts, per_device(): v_piece = lax.all_gather(values, 'seq', axis=0, tiled=True)  2.93 us
  transfers between devices with their start and end apart: 2, of which 2 were waited for; matrix products, arithmetic and copies ran while one was open for 24% of the time, Pallas kernels for 0%

commit v1 on v0

--- a/solution.py
+++ b/solution.py
@@ -51,7 +51,12 @@
     query_doc = doc_place(own_pos, doc_lengths)[0]
     q_heads = q_rot.reshape(row_count, KV_HEADS, group_size, HEAD_DIM)
     k_piece = lax.all_gather(k_rot, "seq", axis=0, tiled=True)
-    v_piece = lax.all_gather(values, "seq", axis=0, tiled=True)
+    ring = [values]
+    for hop in range(15):
+        ring.append(lax.ppermute(ring[-1], "seq", [(dev, (dev + 1) % 16) for dev in range(16)]))
+    v_piece = jnp.roll(
+        jnp.concatenate(ring[::-1], axis=0), (lax.axis_index("seq") + 1) * ring[0].shape[0], axis=0
+    )
     length = k_piece.shape[0]
     key_pos = jnp.arange(length, dtype=jnp.int32)
     key_doc = doc_place(key_pos, doc_lengths)[0]

time: 121 us -> 178 us (1.47)
  waiting for transfers between devices: 57.5 us -> 108 us
  local copies, waits for them, and re-layouts: 6.76 us -> 11.4 us
    ppermute x0 -> x15, waiting for transfers between devices: none -> 102 us  [per_device(): lax.ppermute(ring[-1], 'seq', [(dev, (dev + 1) % 16) for dev in range(16)])]
    all_gather x1, waiting for transfers between devices: 40.6 us -> 5.97 us  [per_device(): k_piece = lax.all_gather(k_rot, 'seq', axis=0, tiled=True)]
    all_gather x1 -> x0, waiting for transfers between devices: 16.2 us -> none  [per_device(): v_piece = lax.all_gather(values, 'seq', axis=0, tiled=True)]
    unnamed x1 -> x48, local copies, waits for them, and re-layouts: 1.55 us -> 6.45 us
    all_gather x1 -> x0, local copies, waits for them, and re-layouts: 2.93 us -> none  [per_device(): v_piece = lax.all_gather(values, 'seq', axis=0, tiled=True)]
    dynamic_slice x0 -> x2, local copies, waits for them, and re-layouts: none -> 2.63 us  [per_device(): jnp.roll(jnp.concatenate(ring[::-1], axis=0), (lax.axis_index('seq') + 1)...]
  transfers between devices with their start and end apart: 2 -> 16, of which waited for: 2 -> 16; matrix products, arithmetic and copies ran while one was open for 24% -> 8% of each run, Pallas kernels for 0% -> 0%
where the time goes in v1:
time: 178 us; the launch traced here: 177 us
  waiting for transfers between devices  108 us (61%)
  matrix products  26.3 us (15%)
  other arithmetic  16.8 us (9%)
  between operations  13.8 us (8%)
  local copies, waits for them, and re-layouts  11.4 us (6%)
    ppermute x15, waiting for transfers between devices, per_device(): lax.ppermute(ring[-1], 'seq', [(dev, (dev + 1) % 16) for dev in range(16)])  102 us
    reduce_sum x1, other arithmetic, per_device(): weight_sum = jnp.sum(weight, axis=-1)  13.3 us
    dot_general x1, matrix products, per_device(): jnp.einsum('qkgs,skd->qkgd', weight.astype(jnp.bfloat16), v_heads, prefer...  13.2 us
    dot_general x1, matrix products, per_device(): jnp.einsum('qkgd,skd->qkgs', q_heads, k_heads, preferred_element_type=jnp...  13.1 us
    unnamed x48, local copies, waits for them, and re-layouts  6.45 us
    all_gather x1, waiting for transfers between devices, per_device(): k_piece = lax.all_gather(k_rot, 'seq', axis=0, tiled=True)  5.97 us
  transfers between devices with their start and end apart: 16, of which 16 were waited for; matrix products, arithmetic and copies ran while one was open for 8% of the time, Pallas kernels for 0%

profile of v1, /device:TPU:0, one launch (start us, length us, event | category | flops | bytes accessed | tf_op | source)
XLA Modules:
  0.0 177.2 jit_solution(17972475519825413711)
XLA Ops:
  6.5 0.0 all-gather.2.cloned.1.call-start
  6.5 0.5 collective-permute-start
  7.0 7.8 %collective-permute-done = bf16[128,512]{1,0:T(8,128)(2,1)S(1)} collective-permute-done((bf16[128,512]{1,0:T(8,128)(2,1)}, bf16[128,512]{1,0:T(8,128)(2,1)S(1)}, u32[]{:S(2)}, u32[]{:S(2)}) %collective-permute-start) | collective-permute-done | bytes 131104 | tf_op jit(solution)/shard_map/ppermute | solution.py:56
  14.9 0.0 collective-permute-start.1
  14.9 7.1 %collective-permute-done.1 = bf16[128,512]{1,0:T(8,128)(2,1)S(1)} collective-permute-done((bf16[128,512]{1,0:T(8,128)(2,1)S(1)}, bf16[128,512]{1,0:T(8,128)(2,1)S(1)}, u32[]{:S(2)}, u32[]{:S(2)}) %collective-permute-start.1) | collective-permute-done | bytes 131104 | tf_op jit(solution)/shard_map/ppermute | solution.py:56
  22.0 0.0 collective-permute-start.2
  22.0 7.1 %collective-permute-done.2 = bf16[128,512]{1,0:T(8,128)(2,1)S(1)} collective-permute-done((bf16[128,512]{1,0:T(8,128)(2,1)S(1)}, bf16[128,512]{1,0:T(8,128)(2,1)S(1)}, u32[]{:S(2)}, u32[]{:S(2)}) %collective-permute-start.2) | collective-permute-done | bytes 131104 | tf_op jit(solution)/shard_map/ppermute | solution.py:56
  29.1 0.0 collective-permute-start.3
  29.1 7.1 %collective-permute-done.3 = bf16[128,512]{1,0:T(8,128)(2,1)S(1)} collective-permute-done((bf16[128,512]{1,0:T(8,128)(2,1)S(1)}, bf16[128,512]{1,0:T(8,128)(2,1)S(1)}, u32[]{:S(2)}, u32[]{:S(2)}) %collective-permute-start.3) | collective-permute-done | bytes 131104 | tf_op jit(solution)/shard_map/ppermute | solution.py:56
  36.1 0.0 collective-permute-start.4
  36.1 7.1 %collective-permute-done.4 = bf16[128,512]{1,0:T(8,128)(2,1)S(1)} collective-permute-done((bf16[128,512]{1,0:T(8,128)(2,1)S(1)}, bf16[128,512]{1,0:T(8,128)(2,1)S(1)}, u32[]{:S(2)}, u32[]{:S(2)}) %collective-permute-start.4) | collective-permute-done | bytes 131104 | tf_op jit(solution)/shard_map/ppermute | solution.py:56
  43.2 0.0 collective-permute-start.5
  43.2 7.1 %collective-permute-done.5 = bf16[128,512]{1,0:T(8,128)(2,1)S(1)} collective-permute-done((bf16[128,512]{1,0:T(8,128)(2,1)S(1)}, bf16[128,512]{1,0:T(8,128)(2,1)S(1)}, u32[]{:S(2)}, u32[]{:S(2)}) %collective-permute-start.5) | collective-permute-done | bytes 131104 | tf_op jit(solution)/shard_map/ppermute | solution.py:56
  50.3 0.0 collective-permute-start.6
  50.3 7.1 %collective-permute-done.6 = bf16[128,512]{1,0:T(8,128)(2,1)S(1)} collective-permute-done((bf16[128,512]{1,0:T(8,128)(2,1)S(1)}, bf16[128,512]{1,0:T(8,128)(2,1)S(1)}, u32[]{:S(2)}, u32[]{:S(2)}) %collective-permute-start.6) | collective-permute-done | bytes 131104 | tf_op jit(solution)/shard_map/ppermute | solution.py:56
  57.4 0.0 collective-permute-start.7
  57.4 0.8 reduce-window.8
  58.3 0.7 fusion.10
  59.0 5.5 %collective-permute-done.7 = bf16[128,512]{1,0:T(8,128)(2,1)S(1)} collective-permute-done((bf16[128,512]{1,0:T(8,128)(2,1)S(1)}, bf16[128,512]{1,0:T(8,128)(2,1)S(1)}, u32[]{:S(2)}, u32[]{:S(2)}) %collective-permute-start.7) | collective-permute-done | bytes 131104 | tf_op jit(solution)/shard_map/ppermute | solution.py:56
  64.5 0.0 collective-permute-start.8
  64.5 1.0 copy.31
  65.5 6.1 %collective-permute-done.8 = bf16[128,512]{1,0:T(8,128)(2,1)S(1)} collective-permute-done((bf16[128,512]{1,0:T(8,128)(2,1)S(1)}, bf16[128,512]{1,0:T(8,128)(2,1)S(1)}, u32[]{:S(2)}, u32[]{:S(2)}) %collective-permute-start.8) | collective-permute-done | bytes 131104 | tf_op jit(solution)/shard_map/ppermute | solution.py:56
  71.6 0.0 collective-permute-start.9
  71.6 0.2 multiply_cosine_fusion
  71.8 6.9 %collective-permute-done.9 = bf16[128,512]{1,0:T(8,128)(2,1)S(1)} collective-permute-done((bf16[128,512]{1,0:T(8,128)(2,1)S(1)}, bf16[128,512]{1,0:T(8,128)(2,1)S(1)}, u32[]{:S(2)}, u32[]{:S(2)}) %collective-permute-start.9) | collective-permute-done | bytes 131104 | tf_op jit(solution)/shard_map/ppermute | solution.py:56
  78.7 0.0 collective-permute-start.10
  78.7 7.0 %collective-permute-done.10 = bf16[128,512]{1,0:T(8,128)(2,1)S(1)} collective-permute-done((bf16[128,512]{1,0:T(8,128)(2,1)S(1)}, bf16[128,512]{1,0:T(8,128)(2,1)S(1)}, u32[]{:S(2)}, u32[]{:S(2)}) %collective-permute-start.10) | collective-permute-done | bytes 131104 | tf_op jit(solution)/shard_map/ppermute | solution.py:56
  85.8 0.0 collective-permute-start.11
  85.8 0.7 pad_maximum_fusion.1
  86.5 0.0 all-gather.2.cloned.1.call-update
  86.5 0.1 convert_reduce_fusion
  86.6 6.3 %collective-permute-done.11 = bf16[128,512]{1,0:T(8,128)(2,1)S(1)} collective-permute-done((bf16[128,512]{1,0:T(8,128)(2,1)S(1)}, bf16[128,512]{1,0:T(8,128)(2,1)S(1)}, u32[]{:S(2)}, u32[]{:S(2)}) %collective-permute-start.11) | collective-permute-done | bytes 131104 | tf_op jit(solution)/shard_map/ppermute | solution.py:56
  92.9 0.0 collective-permute-start.12
  92.9 0.3 fusion.9
  93.2 1.6 copy.21
  94.8 0.2 convert.18
  95.0 0.0 copy-start.1
  95.0 5.1 %collective-permute-done.12 = bf16[128,512]{1,0:T(8,128)(2,1)S(1)} collective-permute-done((bf16[128,512]{1,0:T(8,128)(2,1)S(1)}, bf16[128,512]{1,0:T(8,128)(2,1)S(1)}, u32[]{:S(2)}, u32[]{:S(2)}) %collective-permute-start.12) | collective-permute-done | bytes 131104 | tf_op jit(solution)/shard_map/ppermute | solution.py:56
  100.1 0.0 collective-permute-start.13
  100.1 0.3 subtract_convert_fusion
  100.4 8.0 %collective-permute-done.13 = bf16[128,512]{1,0:T(8,128)(2,1)} collective-permute-done((bf16[128,512]{1,0:T(8,128)(2,1)S(1)}, bf16[128,512]{1,0:T(8,128)(2,1)}, u32[]{:S(2)}, u32[]{:S(2)}) %collective-permute-start.13) | collective-permute-done | bytes 131104 | tf_op jit(solution)/shard_map/ppermute | solution.py:56
  108.3 0.0 collective-permute-start.14
  108.3 0.0 copy-done.2
  108.3 0.0 copy-done.4
  108.3 0.0 copy-done.6
  108.3 0.0 copy-start.7
  108.4 0.0 copy-start.5
  108.4 0.0 copy-start.3
  108.4 0.1 pad_maximum_fusion
  108.4 7.2 %collective-permute-done.14 = bf16[128,512]{1,0:T(8,128)(2,1)S(1)} collective-permute-done((bf16[128,512]{1,0:T(8,128)(2,1)}, bf16[128,512]{1,0:T(8,128)(2,1)S(1)}, u32[]{:S(2)}, u32[]{:S(2)}) %collective-permute-start.14) | collective-permute-done | bytes 131104 | tf_op jit(solution)/shard_map/ppermute | solution.py:56
  115.7 0.9 constant_dynamic-update-slice_fusion.30
  116.6 0.9 constant_dynamic-update-slice_fusion.29
  117.5 0.9 constant_dynamic-update-slice_fusion.28
  118.4 0.9 constant_dynamic-update-slice_fusion.27
  119.5 0.0 copy-done.1
  119.6 0.9 constant_dynamic-update-slice_fusion.14
  120.8 0.1 constant_dynamic-slice_fusion
  120.9 2.5 %copy.18 = bf16[2048,512]{0,1:T(8,128)(2,1)} copy(bf16[2048,512]{1,0:T(8,128)(2,1)S(1)} %constant_dynamic-slice_fusion) | data formatting | bytes 4194304 | tf_op jit(solution)/shard_map/jit(_roll_dynamic)/dynamic_slice | solution.py:57
  123.4 6.0 %all-gather.2.cloned.1.call-done = bf16[2048,512]{0,1:T(8,128)(2,1)} async-done(((bf16[128,512]{0,1:T(8,128)(2,1)}), bf16[2048,512]{0,1:T(8,128)(2,1)}) %all-gather.2.cloned.1.call-update) | async-done | bytes 2097168 | tf_op jit(solution)/shard_map/all_gather | solution.py:53
  129.4 13.1 %fusion = (f32[128,4,7]{0,2,1:T(8,128)S(1)}, f32[4,2048,128,7]{2,1,3,0:T(8,128)}) fusion(pred[128,2048]{0,1:T(8,128)(4,1)S(1)} %fusion.9, bf16[2048,4,128,1]{0,2,3,1:T(8,128)(2,1)} %bitcast.42, bf16[128,4,7,128]{0,3,2,1:T(8,128)(2,1)S(1)} %bitcast.40), kind=kOutput, calls=%fused_computation.2 | convolution fusion | flops 1901064704 | bytes 32651264 | tf_op jit(solution)/shard_map/qkgd,skd->qkgs/dot_general | solution.py:69
  142.5 13.3 %fusion.1 = f32[128,4,7]{0,2,1:T(8,128)S(1)} fusion(f32[4,2048,128,7]{2,1,3,0:T(8,128)} %get-tuple-element.14, f32[128,4,7]{0,2,1:T(8,128)S(1)} %broadcast_maximum_fusion, pred[128,2048]{0,1:T(8,128)(4,1)S(1)} %fusion.9), kind=kLoop, calls=%fused_computation.3 | loop fusion | flops 36696576 | bytes 29650944 | tf_op jit(solution)/shard_map/reduce_sum | solution.py:75
  155.8 0.0 copy-done
  155.8 13.2 %fusion.6 = bf16[128,4,7,128]{0,3,2,1:T(8,128)(2,1)S(1)} fusion(bf16[2048,4,128,1]{0,2,3,1:T(8,128)(2,1)S(1)} %bitcast.41, f32[4,2048,128,7]{2,1,3,0:T(8,128)} %get-tuple-element.14, f32[128,4,7]{0,2,1:T(8,128)S(1)} %broadcast_maximum_fusion, pred[128,2048]{0,1:T(8,128)(4,1)S(1)} %fusion.9, f32[128,4,7]{0,2,1:T(8,128)S(1)} %fusion.1), kind=kOutput, calls=%fused_computation.8 | convolution fusion | flops 1916665856 | bytes 32665600 | tf_op jit(solution)/shard_map/qkgs,skd->qkgd/dot_general | solution.py:76
  169.0 1.3 copy.25
  (39 shorter events, 0.4 us)
Async XLA Ops:
  6.5 122.9 %all-gather.2.cloned.1.call-start = ((), (), s32[]{:S(2)}) async-start(), calls=%async_computation | async-start | bytes 2228224 | tf_op jit(solution)/shard_map/all_gather | solution.py:53
  6.5 8.3 %collective-permute-start = (bf16[128,512]{1,0:T(8,128)(2,1)}, bf16[128,512]{1,0:T(8,128)(2,1)S(1)}, u32[]{:S(2)}, u32[]{:S(2)}) collective-permute-start(bf16[128,512]{1,0:T(8,128)(2,1)} %param.6), channel_id=1, source_target_pairs={{0,2},{2,4},{4,6},{6,8},{8,10},{10,12},{12,14},{14,16},{16,18},{18... | collective-permute-start | bytes 393224 | tf_op jit(solution)/shard_map/ppermute | solution.py:56
  14.9 7.1 %collective-permute-start.1 = (bf16[128,512]{1,0:T(8,128)(2,1)S(1)}, bf16[128,512]{1,0:T(8,128)(2,1)S(1)}, u32[]{:S(2)}, u32[]{:S(2)}) collective-permute-start(bf16[128,512]{1,0:T(8,128)(2,1)S(1)} %collective-permute-done), channel_id=1, source_target_pairs={{0,2},{2,4},{4,6},{6,8},{8,10},{10,12},{12,14},{14,16},{16,18},{18... | collective-permute-start | bytes 393224 | tf_op jit(solution)/shard_map/ppermute | solution.py:56
  22.0 7.1 %collective-permute-start.2 = (bf16[128,512]{1,0:T(8,128)(2,1)S(1)}, bf16[128,512]{1,0:T(8,128)(2,1)S(1)}, u32[]{:S(2)}, u32[]{:S(2)}) collective-permute-start(bf16[128,512]{1,0:T(8,128)(2,1)S(1)} %collective-permute-done.1), channel_id=1, source_target_pairs={{0,2},{2,4},{4,6},{6,8},{8,10},{10,12},{12,14},{14,16},{16,18},{18... | collective-permute-start | bytes 393224 | tf_op jit(solution)/shard_map/ppermute | solution.py:56
  29.1 7.1 %collective-permute-start.3 = (bf16[128,512]{1,0:T(8,128)(2,1)S(1)}, bf16[128,512]{1,0:T(8,128)(2,1)S(1)}, u32[]{:S(2)}, u32[]{:S(2)}) collective-permute-start(bf16[128,512]{1,0:T(8,128)(2,1)S(1)} %collective-permute-done.2), channel_id=1, source_target_pairs={{0,2},{2,4},{4,6},{6,8},{8,10},{10,12},{12,14},{14,16},{16,18},{18... | collective-permute-start | bytes 393224 | tf_op jit(solution)/shard_map/ppermute | solution.py:56
  36.1 7.1 %collective-permute-start.4 = (bf16[128,512]{1,0:T(8,128)(2,1)S(1)}, bf16[128,512]{1,0:T(8,128)(2,1)S(1)}, u32[]{:S(2)}, u32[]{:S(2)}) collective-permute-start(bf16[128,512]{1,0:T(8,128)(2,1)S(1)} %collective-permute-done.3), channel_id=1, source_target_pairs={{0,2},{2,4},{4,6},{6,8},{8,10},{10,12},{12,14},{14,16},{16,18},{18... | collective-permute-start | bytes 393224 | tf_op jit(solution)/shard_map/ppermute | solution.py:56
  43.2 7.1 %collective-permute-start.5 = (bf16[128,512]{1,0:T(8,128)(2,1)S(1)}, bf16[128,512]{1,0:T(8,128)(2,1)S(1)}, u32[]{:S(2)}, u32[]{:S(2)}) collective-permute-start(bf16[128,512]{1,0:T(8,128)(2,1)S(1)} %collective-permute-done.4), channel_id=1, source_target_pairs={{0,2},{2,4},{4,6},{6,8},{8,10},{10,12},{12,14},{14,16},{16,18},{18... | collective-permute-start | bytes 393224 | tf_op jit(solution)/shard_map/ppermute | solution.py:56
  50.3 7.1 %collective-permute-start.6 = (bf16[128,512]{1,0:T(8,128)(2,1)S(1)}, bf16[128,512]{1,0:T(8,128)(2,1)S(1)}, u32[]{:S(2)}, u32[]{:S(2)}) collective-permute-start(bf16[128,512]{1,0:T(8,128)(2,1)S(1)} %collective-permute-done.5), channel_id=1, source_target_pairs={{0,2},{2,4},{4,6},{6,8},{8,10},{10,12},{12,14},{14,16},{16,18},{18... | collective-permute-start | bytes 393224 | tf_op jit(solution)/shard_map/ppermute | solution.py:56
  57.4 7.1 %collective-permute-start.7 = (bf16[128,512]{1,0:T(8,128)(2,1)S(1)}, bf16[128,512]{1,0:T(8,128)(2,1)S(1)}, u32[]{:S(2)}, u32[]{:S(2)}) collective-permute-start(bf16[128,512]{1,0:T(8,128)(2,1)S(1)} %collective-permute-done.6), channel_id=1, source_target_pairs={{0,2},{2,4},{4,6},{6,8},{8,10},{10,12},{12,14},{14,16},{16,18},{18... | collective-permute-start | bytes 393224 | tf_op jit(solution)/shard_map/ppermute | solution.py:56
  64.5 7.1 %collective-permute-start.8 = (bf16[128,512]{1,0:T(8,128)(2,1)S(1)}, bf16[128,512]{1,0:T(8,128)(2,1)S(1)}, u32[]{:S(2)}, u32[]{:S(2)}) collective-permute-start(bf16[128,512]{1,0:T(8,128)(2,1)S(1)} %collective-permute-done.7), channel_id=1, source_target_pairs={{0,2},{2,4},{4,6},{6,8},{8,10},{10,12},{12,14},{14,16},{16,18},{18... | collective-permute-start | bytes 393224 | tf_op jit(solution)/shard_map/ppermute | solution.py:56
  71.6 7.1 %collective-permute-start.9 = (bf16[128,512]{1,0:T(8,128)(2,1)S(1)}, bf16[128,512]{1,0:T(8,128)(2,1)S(1)}, u32[]{:S(2)}, u32[]{:S(2)}) collective-permute-start(bf16[128,512]{1,0:T(8,128)(2,1)S(1)} %collective-permute-done.8), channel_id=1, source_target_pairs={{0,2},{2,4},{4,6},{6,8},{8,10},{10,12},{12,14},{14,16},{16,18},{18... | collective-permute-start | bytes 393224 | tf_op jit(solution)/shard_map/ppermute | solution.py:56
  78.7 7.1 %collective-permute-start.10 = (bf16[128,512]{1,0:T(8,128)(2,1)S(1)}, bf16[128,512]{1,0:T(8,128)(2,1)S(1)}, u32[]{:S(2)}, u32[]{:S(2)}) collective-permute-start(bf16[128,512]{1,0:T(8,128)(2,1)S(1)} %collective-permute-done.9), channel_id=1, source_target_pairs={{0,2},{2,4},{4,6},{6,8},{8,10},{10,12},{12,14},{14,16},{16,18},{18... | collective-permute-start | bytes 393224 | tf_op jit(solution)/shard_map/ppermute | solution.py:56
  85.8 22.5 %copy-start.2 = (bf16[128,512]{1,0:T(8,128)(2,1)}, bf16[128,512]{1,0:T(8,128)(2,1)S(1)}, u32[]{:S(2)}) copy-start(bf16[128,512]{1,0:T(8,128)(2,1)S(1)} %collective-permute-done.10) | copy-start | bytes 393220
  85.8 7.1 %collective-permute-start.11 = (bf16[128,512]{1,0:T(8,128)(2,1)S(1)}, bf16[128,512]{1,0:T(8,128)(2,1)S(1)}, u32[]{:S(2)}, u32[]{:S(2)}) collective-permute-start(bf16[128,512]{1,0:T(8,128)(2,1)S(1)} %collective-permute-done.10), channel_id=1, source_target_pairs={{0,2},{2,4},{4,6},{6,8},{8,10},{10,12},{12,14},{14,16},{16,18},{18... | collective-permute-start | bytes 393224 | tf_op jit(solution)/shard_map/ppermute | solution.py:56
  92.9 15.5 %copy-start.4 = (bf16[128,512]{1,0:T(8,128)(2,1)}, bf16[128,512]{1,0:T(8,128)(2,1)S(1)}, u32[]{:S(2)}) copy-start(bf16[128,512]{1,0:T(8,128)(2,1)S(1)} %collective-permute-done.11) | copy-start | bytes 393220
  92.9 7.2 %collective-permute-start.12 = (bf16[128,512]{1,0:T(8,128)(2,1)S(1)}, bf16[128,512]{1,0:T(8,128)(2,1)S(1)}, u32[]{:S(2)}, u32[]{:S(2)}) collective-permute-start(bf16[128,512]{1,0:T(8,128)(2,1)S(1)} %collective-permute-done.11), channel_id=1, source_target_pairs={{0,2},{2,4},{4,6},{6,8},{8,10},{10,12},{12,14},{14,16},{16,18},{18... | collective-permute-start | bytes 393224 | tf_op jit(solution)/shard_map/ppermute | solution.py:56
  95.0 24.6 %copy-start.1 = (bf16[128,512]{1,0:T(8,128)(2,1)S(1)}, bf16[128,512]{1,0:T(8,128)(2,1)}, u32[]{:S(2)}) copy-start(bf16[128,512]{1,0:T(8,128)(2,1)} %param.6) | copy-start | bytes 393220
  100.1 8.3 %copy-start.6 = (bf16[128,512]{1,0:T(8,128)(2,1)}, bf16[128,512]{1,0:T(8,128)(2,1)S(1)}, u32[]{:S(2)}) copy-start(bf16[128,512]{1,0:T(8,128)(2,1)S(1)} %collective-permute-done.12) | copy-start | bytes 393220
  100.1 8.3 %collective-permute-start.13 = (bf16[128,512]{1,0:T(8,128)(2,1)S(1)}, bf16[128,512]{1,0:T(8,128)(2,1)}, u32[]{:S(2)}, u32[]{:S(2)}) collective-permute-start(bf16[128,512]{1,0:T(8,128)(2,1)S(1)} %collective-permute-done.12), channel_id=1, source_target_pairs={{0,2},{2,4},{4,6},{6,8},{8,10},{10,12},{12,14},{14,16},{16,18},{18... | collective-permute-start | bytes 393224 | tf_op jit(solution)/shard_map/ppermute | solution.py:56
  108.3 7.3 %collective-permute-start.14 = (bf16[128,512]{1,0:T(8,128)(2,1)}, bf16[128,512]{1,0:T(8,128)(2,1)S(1)}, u32[]{:S(2)}, u32[]{:S(2)}) collective-permute-start(bf16[128,512]{1,0:T(8,128)(2,1)} %collective-permute-done.13), channel_id=1, source_target_pairs={{0,2},{2,4},{4,6},{6,8},{8,10},{10,12},{12,14},{14,16},{16,18},{18... | collective-permute-start | bytes 393224 | tf_op jit(solution)/shard_map/ppermute | solution.py:56
  108.3 12.2 %copy-start.7 = (bf16[128,512]{1,0:T(8,128)(2,1)S(1)}, bf16[128,512]{1,0:T(8,128)(2,1)}, u32[]{:S(2)}) copy-start(bf16[128,512]{1,0:T(8,128)(2,1)} %copy-done.6) | copy-start | bytes 393220
  108.4 12.2 %copy-start.5 = (bf16[128,512]{1,0:T(8,128)(2,1)S(1)}, bf16[128,512]{1,0:T(8,128)(2,1)}, u32[]{:S(2)}) copy-start(bf16[128,512]{1,0:T(8,128)(2,1)} %copy-done.4) | copy-start | bytes 393220
  108.4 12.2 %copy-start.3 = (bf16[128,512]{1,0:T(8,128)(2,1)S(1)}, bf16[128,512]{1,0:T(8,128)(2,1)}, u32[]{:S(2)}) copy-start(bf16[128,512]{1,0:T(8,128)(2,1)} %copy-done.2) | copy-start | bytes 393220
  142.5 13.3 %copy-start = (bf16[2048,512]{0,1:T(8,128)(2,1)S(1)}, bf16[2048,512]{0,1:T(8,128)(2,1)}, u32[]{:S(2)}) copy-start(bf16[2048,512]{0,1:T(8,128)(2,1)} %copy.18) | copy-start | bytes 6291460
Sparse Core Ops, SparseCore 0:
  86.6 42.7 all-gather.1
